TPU v7x, 32 devices: a whole 2x2x4 slice. The times are simulated.
32 devices in a mesh: rows: 8 (over z, y), cols: 4 (over x, core).
Axes of the slice: x: 2, y: 2, z: 4, core: 2. Of those that a mesh axis runs over, the one named last changes fastest.
Arguments:
- gradient: float32 [8192, 29568], P('rows', 'cols'), as said below
- start_block: float32 [29568, 64], P('cols'), may hold values from -0.03125 to 0.03125
- activations: float32 [512, 29568], P('rows', 'cols'), may hold values from -6 to 6
- out_grads: float32 [512, 8192], P('rows', 'cols'), may hold values from -6 to 6
Outputs:
- left_factor: float32 [8192, 64], P('rows')
- right_factor: float32 [29568, 64], P('cols')
- scores: float32 [512], P('rows')
Inputs may be any that keep to these rules, and one draw needn't show every extreme that they name: real-valued gradient entries, of order 29568 ** -0.5.
All inputs are finite; a program needn't handle non-finite values.
Results may differ from a plain program's by a relative error of at most 0.00013.
Values sent between devices are 32-bit elements; how exact they have to be, the bound alone decides.
A program may use at most 128 MiB of HBM per device.

v0:
```python
import jax
import jax.numpy as jnp
from jax import lax
from jax.sharding import PartitionSpec as P

ITERS = 2
HIGH = lax.Precision.HIGHEST


def factor_with(block, gram):
    lower = jnp.linalg.cholesky(gram)
    return (
        lax.linalg.triangular_solve(lower, block, left_side=False, lower=True, transpose_a=True),
        lower,
    )


def inner_gram(block):
    return jnp.dot(block.T, block, precision=HIGH, preferred_element_type=jnp.float32)


def per_device(gradient, start_block, activations, out_grads):
    grad_cols = out_grads.shape[1]
    col_index = lax.axis_index("cols")
    omega = start_block
    for step in range(ITERS):
        ysum = lax.psum(
            jnp.dot(gradient, omega, precision=HIGH, preferred_element_type=jnp.float32), "cols"
        )
        gram = lax.psum(inner_gram(ysum), "rows")
        left, lower_y = factor_with(ysum, gram)
        partial_z = jnp.dot(gradient.T, left, precision=HIGH, preferred_element_type=jnp.float32)
        zsum = lax.psum(partial_z, "rows")
        zgram = lax.psum(inner_gram(zsum), "cols")
        right, lower_z = factor_with(zsum, zgram)
        omega = right
    whole_rows = lax.all_gather(left, "rows", axis=0, tiled=True)
    left_cols = lax.dynamic_slice_in_dim(whole_rows, col_index * grad_cols, grad_cols, 0)
    left_part = jnp.dot(out_grads, left_cols, precision=HIGH, preferred_element_type=jnp.float32)
    right_part = jnp.dot(activations, right, precision=HIGH, preferred_element_type=jnp.float32)
    token_left, token_right = lax.psum((left_part, right_part), "cols")
    mixed = jnp.dot(token_left, lower_z, precision=HIGH, preferred_element_type=jnp.float32)
    scores = jnp.sum(mixed * token_right, axis=1)
    return (left, right, scores)


def solution(mesh):
    placed = (P("rows", "cols"), P("cols", None), P("rows", "cols"), P("rows", "cols"))
    return jax.shard_map(
        per_device,
        mesh=mesh,
        in_specs=placed,
        out_specs=(P("rows", None), P("cols", None), P("rows")),
        check_vma=False,
    )
```

profile of v0, /device:TPU:0, one launch (start us, length us, event | category | flops | bytes accessed | tf_op | source)
XLA Modules:
  0.0 579.3 jit_solution(6776016720726716855)
XLA Ops:
  8.7 24.2 %fusion.23 = f32[1024,64]{0,1:T(8,128)} fusion(f32[1024,7392]{0,1:T(8,128)} %param.9, f32[7392,64]{0,1:T(8,128)S(1)} %copy-done), kind=kOutput, calls=%fused_computation.50 | convolution fusion | flops 5813305344 | bytes 32432128 | tf_op jit(solution)/shard_map/dot_general | solution.py:28
  33.0 35.1 %all-reduce.6.cloned.1.call-done = f32[1024,64]{0,1:T(8,128)} async-done(((f32[1024,64]{0,1:T(8,128)}), f32[1024,64]{0,1:T(8,128)}) %all-reduce.6.cloned.1.call-update) | async-done | bytes 262160 | tf_op jit(solution)/shard_map/psum | solution.py:27
  69.5 37.5 %psum.71 = f32[64,64]{0,1:T(8,128)S(1)} all-reduce(f32[64,64]{0,1:T(8,128)S(1)} %fusion.24), channel_id=1, replica_groups=mesh['rows'=8,'cols'=4] {'rows'}, use_global_device_ids=true, to_apply=%region_1.0 | all-reduce | flops 4096 | bytes 32768 | tf_op jit(solution)/shard_map/psum | solution.py:30
  107.1 5.8 %cholesky.74 = f32[64,64]{1,0:T(8,128)S(1)} custom-call(f32[64,64]{1,0:T(8,128)S(1)} %fusion.12), custom_call_target="Cholesky" | custom-call | tf_op jit(solution)/shard_map/jit(cholesky)/cholesky | solution.py:11
  114.3 4.9 custom-call.10
  120.6 30.9 %convolution_bitcast_fusion.3 = f32[7392,64]{0,1:T(8,128)} fusion(f32[1024,64]{0,1:T(8,128)S(1)} %convolution_bitcast_fusion.5, f32[1024,7392]{0,1:T(8,128)} %param.9), kind=kOutput, calls=%fused_computation.3 | convolution fusion | flops 5813305344 | bytes 32432128 | tf_op jit(solution)/shard_map/dot_general | solution.py:32
  151.5 93.6 %all-reduce.8.cloned.1.call-done = f32[7392,64]{0,1:T(8,128)} async-done(((f32[7392,64]{0,1:T(8,128)}), f32[7392,64]{0,1:T(8,128)}) %all-reduce.8.cloned.1.call-update) | async-done | bytes 1892368 | tf_op jit(solution)/shard_map/psum | solution.py:33
  245.1 3.8 fusion.25
  248.9 11.9 %psum.73 = f32[64,64]{0,1:T(8,128)S(1)} all-reduce(f32[64,64]{0,1:T(8,128)S(1)} %fusion.25), channel_id=1, replica_groups=mesh['rows'=8,'cols'=4] {'cols'}, use_global_device_ids=true, to_apply=%region_5.8 | all-reduce | flops 4096 | bytes 32768 | tf_op jit(solution)/shard_map/psum | solution.py:34
  260.9 5.8 %cholesky.85 = f32[64,64]{1,0:T(8,128)S(1)} custom-call(f32[64,64]{1,0:T(8,128)S(1)} %fusion.10), custom_call_target="Cholesky" | custom-call | tf_op jit(solution)/shard_map/jit(cholesky)/cholesky | solution.py:11
  268.1 4.9 custom-call.11
  276.2 23.1 %convolution_bitcast_fusion.6 = f32[1024,64]{0,1:T(8,128)} fusion(f32[7392,64]{0,1:T(8,128)S(1)} %convolution_bitcast_fusion.2, f32[1024,7392]{0,1:T(8,128)} %param.9), kind=kOutput, calls=%fused_computation.6 | convolution fusion | flops 5813305344 | bytes 32432128 | tf_op jit(solution)/shard_map/dot_general | solution.py:28
  299.4 31.0 %all-reduce.10.cloned.1.call-done = f32[1024,64]{0,1:T(8,128)} async-done(((f32[1024,64]{0,1:T(8,128)}), f32[1024,64]{0,1:T(8,128)}) %all-reduce.10.cloned.1.call-update) | async-done | bytes 262160 | tf_op jit(solution)/shard_map/psum | solution.py:27
  331.9 37.4 %psum.75 = f32[64,64]{0,1:T(8,128)S(1)} all-reduce(f32[64,64]{0,1:T(8,128)S(1)} %fusion.26), channel_id=1, replica_groups=mesh['rows'=8,'cols'=4] {'rows'}, use_global_device_ids=true, to_apply=%region_7.11 | all-reduce | flops 4096 | bytes 32768 | tf_op jit(solution)/shard_map/psum | solution.py:30
  369.4 5.8 %cholesky.96 = f32[64,64]{1,0:T(8,128)S(1)} custom-call(f32[64,64]{1,0:T(8,128)S(1)} %fusion.8), custom_call_target="Cholesky" | custom-call | tf_op jit(solution)/shard_map/jit(cholesky)/cholesky | solution.py:11
  376.6 4.9 custom-call.12
  382.9 31.0 %convolution_bitcast_fusion.1 = f32[7392,64]{0,1:T(8,128)} fusion(f32[1024,64]{0,1:T(8,128)S(1)} %convolution_bitcast_fusion.4, f32[1024,7392]{0,1:T(8,128)} %param.9), kind=kOutput, calls=%fused_computation.1 | convolution fusion | flops 5813305344 | bytes 32432128 | tf_op jit(solution)/shard_map/dot_general | solution.py:32
  414.5 93.0 %all-reduce.12.cloned.1.call-done = f32[7392,64]{0,1:T(8,128)} async-done(((f32[7392,64]{0,1:T(8,128)}), f32[7392,64]{0,1:T(8,128)}) %all-reduce.12.cloned.1.call-update) | async-done | bytes 1892368 | tf_op jit(solution)/shard_map/psum | solution.py:33
  507.4 3.8 fusion.27
  511.2 11.6 %psum.77 = f32[64,64]{0,1:T(8,128)S(1)} all-reduce(f32[64,64]{0,1:T(8,128)S(1)} %fusion.27), channel_id=1, replica_groups=mesh['rows'=8,'cols'=4] {'cols'}, use_global_device_ids=true, to_apply=%region_9.13 | all-reduce | flops 4096 | bytes 32768 | tf_op jit(solution)/shard_map/psum | solution.py:34
  522.9 5.8 %cholesky.107 = f32[64,64]{1,0:T(8,128)S(1)} custom-call(f32[64,64]{1,0:T(8,128)S(1)} %fusion.6), custom_call_target="Cholesky" | custom-call | tf_op jit(solution)/shard_map/jit(cholesky)/cholesky | solution.py:11
  530.0 4.9 custom-call.13
  541.3 17.6 %all-gather.2.cloned.1.call-done = f32[8192,64]{0,1:T(8,128)} async-done(((f32[1024,64]{0,1:T(8,128)}), f32[8192,64]{0,1:T(8,128)}) %all-gather.2.cloned.1.call-update) | async-done | bytes 2097168 | tf_op jit(solution)/shard_map/all_gather | solution.py:37
  560.5 10.7 %all-reduce = (f32[64,64]{0,1:T(8,128)S(1)}, f32[64,64]{0,1:T(8,128)S(1)}) all-reduce(f32[64,64]{0,1:T(8,128)S(1)} %convolution_bitcast_fusion.7, f32[64,64]{0,1:T(8,128)S(1)} %convolution_bitcast_fusion.8), channel_id=1, replica_groups=mesh['rows'=8,'cols'=4] {'cols'}, use_global_device_ids=true, to_apply=%region_11.15 | all-reduce | flops 8192 | bytes 65536 | tf_op jit(solution)/shard_map/psum | solution.py:41
  (49 shorter events, 25.9 us)
Async XLA Ops:
  7.2 1.5 copy-start
  7.2 60.9 %all-reduce.6.cloned.1.call-start = ((), (), s32[]{:S(2)}) async-start(), calls=%async_computation | async-start | bytes 524288 | tf_op jit(solution)/shard_map/psum | solution.py:27
  32.9 212.2 %all-reduce.8.cloned.1.call-start = ((), (), s32[]{:S(2)}) async-start(), calls=%async_computation.1 | async-start | bytes 3801088 | tf_op jit(solution)/shard_map/psum | solution.py:33
  151.5 179.0 %all-reduce.10.cloned.1.call-start = ((), (), s32[]{:S(2)}) async-start(), calls=%async_computation.2 | async-start | bytes 524288 | tf_op jit(solution)/shard_map/psum | solution.py:27
  299.4 208.0 %all-reduce.12.cloned.1.call-start = ((), (), s32[]{:S(2)}) async-start(), calls=%async_computation.3 | async-start | bytes 3801088 | tf_op jit(solution)/shard_map/psum | solution.py:33
  382.8 31.0 %copy-start.2 = (f32[1024,64]{0,1:T(8,128)}, f32[1024,64]{0,1:T(8,128)S(1)}, u32[]{:S(2)}) copy-start(f32[1024,64]{0,1:T(8,128)S(1)} %convolution_bitcast_fusion.4) | copy-start | bytes 786436
  413.9 145.0 %all-gather.2.cloned.1.call-start = ((), (), s32[]{:S(2)}) async-start(), calls=%async_computation.4 | async-start | bytes 2359296 | tf_op jit(solution)/shard_map/all_gather | solution.py:37
  534.9 4.7 copy-start.3
  538.3 1.3 copy-start.1
  539.6 19.3 %copy-start.4 = (f32[64,2048]{1,0:T(8,128)S(1)}, f32[64,2048]{1,0:T(8,128)}, u32[]{:S(2)}) copy-start(f32[64,2048]{1,0:T(8,128)} %param.12) | copy-start | bytes 1572868
Sparse Core Ops, SparseCore 0:
  33.0 35.0 all-reduce.5
  151.6 93.4 all-reduce.7
  299.5 30.9 all-reduce.9
  414.0 93.4 all-reduce.11
  510.1 48.7 all-gather.1
where the time goes:
time: 583 us; the launch traced here: 579 us
  waiting for transfers between devices  271 us (46%)
  matrix products  133 us (23%)
  blocking collectives  109 us (19%)
  other arithmetic  48.2 us (8%)
  between operations  14.2 us (2%)
    psum x2, waiting for transfers between devices, per_device(): zsum = lax.psum(partial_z, 'rows')  187 us
    psum x2, blocking collectives, per_device(): gram = lax.psum(inner_gram(ysum), 'rows')  74.9 us
    psum x2, waiting for transfers between devices, per_device(): lax.psum(jnp.dot(gradient, omega, precision=HIGH, preferred_element_type=...  66.2 us
    dot_general x2, matrix products, per_device(): jnp.dot(gradient.T, left, precision=HIGH, preferred_element_type=jnp.floa...  61.9 us
    dot_general x2, matrix products, per_device(): jnp.dot(gradient, omega, precision=HIGH, preferred_element_type=jnp.float32)  47.3 us
    another operation x12, other arithmetic, factor_with(): lower = jnp.linalg.cholesky(gram)  26.1 us
    psum x2, blocking collectives, per_device(): zgram = lax.psum(inner_gram(zsum), 'cols')  23.5 us
    another operation x8, other arithmetic, factor_with(): lax.linalg.triangular_solve(lower, block, left_side=False, lower=True, tr...  22.1 us
  transfers between devices with their start and end apart: 5, of which 5 were waited for; matrix products, arithmetic and copies ran while one was open for 4% of the time, Pallas kernels for 0%

commit v1 on v0

--- a/solution.py
+++ b/solution.py
@@ -30,7 +30,8 @@
         gram = lax.psum(inner_gram(ysum), "rows")
         left, lower_y = factor_with(ysum, gram)
         partial_z = jnp.dot(gradient.T, left, precision=HIGH, preferred_element_type=jnp.float32)
-        zsum = lax.psum(partial_z, "rows")
+        terms = lax.all_gather(partial_z, "rows")
+        zsum = jnp.sum(terms, axis=0)
         zgram = lax.psum(inner_gram(zsum), "cols")
         right, lower_z = factor_with(zsum, zgram)
         omega = right

time: 583 us -> 811 us (1.39)
  waiting for transfers between devices: 271 us -> 488 us
  other arithmetic: 48.2 us -> 61 us
    all_gather x0 -> x2, waiting for transfers between devices: none -> 412 us  [per_device(): terms = lax.all_gather(partial_z, 'rows')]
    psum x2 -> x0, waiting for transfers between devices: 187 us -> none  [per_device(): zsum = lax.psum(partial_z, 'rows')]
    reduce_sum x0 -> x2, other arithmetic: none -> 12.6 us  [per_device(): zsum = jnp.sum(terms, axis=0)]
  transfers between devices with their start and end apart: 5 -> 5, of which waited for: 5 -> 5; matrix products, arithmetic and copies ran while one was open for 4% -> 5% of each run, Pallas kernels for 0% -> 0%
where the time goes in v1:
time: 811 us; the launch traced here: 807 us
  waiting for transfers between devices  488 us (60%)
  matrix products  133 us (16%)
  blocking collectives  107 us (13%)
  other arithmetic  61 us (8%)
  between operations  14.3 us (2%)
    all_gather x2, waiting for transfers between devices, per_device(): terms = lax.all_gather(partial_z, 'rows')  412 us
    psum x2, blocking collectives, per_device(): gram = lax.psum(inner_gram(ysum), 'rows')  74.6 us
    dot_general x2, matrix products, per_device(): jnp.dot(gradient.T, left, precision=HIGH, preferred_element_type=jnp.floa...  66.2 us
    psum x2, waiting for transfers between devices, per_device(): lax.psum(jnp.dot(gradient, omega, precision=HIGH, preferred_element_type=...  65.8 us
    dot_general x2, matrix products, per_device(): jnp.dot(gradient, omega, precision=HIGH, preferred_element_type=jnp.float32)  47.3 us
    another operation x12, other arithmetic, factor_with(): lower = jnp.linalg.cholesky(gram)  26.2 us
    another operation x8, other arithmetic, factor_with(): lax.linalg.triangular_solve(lower, block, left_side=False, lower=True, tr...  22.3 us
    psum x2, blocking collectives, per_device(): zgram = lax.psum(inner_gram(zsum), 'cols')  21.3 us
  transfers between devices with their start and end apart: 5, of which 5 were waited for; matrix products, arithmetic and copies ran while one was open for 5% of the time, Pallas kernels for 0%

profile of v1, /device:TPU:0, one launch (start us, length us, event | category | flops | bytes accessed | tf_op | source)
XLA Modules:
  0.0 806.7 jit_solution(7059181469929115836)
XLA Ops:
  8.7 24.2 %fusion.23 = f32[1024,64]{0,1:T(8,128)} fusion(f32[1024,7392]{0,1:T(8,128)} %param.9, f32[7392,64]{0,1:T(8,128)S(1)} %copy-done), kind=kOutput, calls=%fused_computation.50 | convolution fusion | flops 5813305344 | bytes 32432128 | tf_op jit(solution)/shard_map/dot_general | solution.py:28
  33.0 35.1 %all-reduce.4.cloned.1.call-done = f32[1024,64]{0,1:T(8,128)} async-done(((f32[1024,64]{0,1:T(8,128)}), f32[1024,64]{0,1:T(8,128)}) %all-reduce.4.cloned.1.call-update) | async-done | bytes 262160 | tf_op jit(solution)/shard_map/psum | solution.py:27
  69.5 37.5 %psum.57 = f32[64,64]{0,1:T(8,128)S(1)} all-reduce(f32[64,64]{0,1:T(8,128)S(1)} %fusion.24), channel_id=1, replica_groups=mesh['rows'=8,'cols'=4] {'rows'}, use_global_device_ids=true, to_apply=%region_1.0 | all-reduce | flops 4096 | bytes 32768 | tf_op jit(solution)/shard_map/psum | solution.py:30
  107.1 5.8 cholesky.74
  114.2 4.9 custom-call.10
  120.5 30.9 %convolution_bitcast_fusion.3 = f32[1,7392,64]{1,2,0:T(8,128)} fusion(f32[1024,64]{0,1:T(8,128)S(1)} %convolution_bitcast_fusion.5, f32[1024,7392]{0,1:T(8,128)} %param.9), kind=kOutput, calls=%fused_computation.3 | convolution fusion | flops 5813305344 | bytes 32432128 | tf_op jit(solution)/shard_map/dot_general | solution.py:32
  151.5 204.4 %all-gather.10.cloned.1.call-done = f32[8,7392,64]{1,2,0:T(8,128)} async-done(((f32[1,7392,64]{1,2,0:T(8,128)}), f32[8,7392,64]{1,2,0:T(8,128)}) %all-gather.10.cloned.1.call-update) | async-done | bytes 15138832 | tf_op jit(solution)/shard_map/all_gather | solution.py:33
  355.9 6.3 reduce_sum.27
  363.8 10.9 %psum.58 = f32[64,64]{0,1:T(8,128)S(1)} all-reduce(f32[64,64]{0,1:T(8,128)S(1)} %fusion.25), channel_id=1, replica_groups=mesh['rows'=8,'cols'=4] {'cols'}, use_global_device_ids=true, to_apply=%region_5.8 | all-reduce | flops 4096 | bytes 32768 | tf_op jit(solution)/shard_map/psum | solution.py:35
  374.8 5.8 cholesky.85
  382.0 4.9 custom-call.11
  388.7 23.1 %convolution_bitcast_fusion.6 = f32[1024,64]{0,1:T(8,128)} fusion(f32[7392,64]{0,1:T(8,128)S(1)} %convolution_bitcast_fusion.2, f32[1024,7392]{0,1:T(8,128)} %param.9), kind=kOutput, calls=%fused_computation.6 | convolution fusion | flops 5813305344 | bytes 32432128 | tf_op jit(solution)/shard_map/dot_general | solution.py:28
  411.9 30.7 %all-reduce.6.cloned.1.call-done = f32[1024,64]{0,1:T(8,128)} async-done(((f32[1024,64]{0,1:T(8,128)}), f32[1024,64]{0,1:T(8,128)}) %all-reduce.6.cloned.1.call-update) | async-done | bytes 262160 | tf_op jit(solution)/shard_map/psum | solution.py:27
  444.0 37.1 %psum.60 = f32[64,64]{0,1:T(8,128)S(1)} all-reduce(f32[64,64]{0,1:T(8,128)S(1)} %fusion.26), channel_id=1, replica_groups=mesh['rows'=8,'cols'=4] {'rows'}, use_global_device_ids=true, to_apply=%region_7.11 | all-reduce | flops 4096 | bytes 32768 | tf_op jit(solution)/shard_map/psum | solution.py:30
  481.2 5.9 cholesky.96
  488.4 4.9 custom-call.12
  495.6 35.3 %convolution_bitcast_fusion.1 = f32[1,7392,64]{1,2,0:T(8,128)} fusion(f32[1024,64]{0,1:T(8,128)} %convolution_bitcast_fusion.4, f32[1024,7392]{0,1:T(8,128)} %param.9), kind=kOutput, calls=%fused_computation.1 | convolution fusion | flops 5813305344 | bytes 32432128 | tf_op jit(solution)/shard_map/dot_general | solution.py:32
  530.9 10.0 %all-gather.8.cloned.1.call-done = f32[8192,64]{0,1:T(8,128)} async-done(((f32[1024,64]{0,1:T(8,128)}), f32[8192,64]{0,1:T(8,128)}) %all-gather.8.cloned.1.call-update) | async-done | bytes 2097168 | tf_op jit(solution)/shard_map/all_gather | solution.py:38
  542.5 207.6 %all-gather.12.cloned.1.call-done = f32[8,7392,64]{1,2,0:T(8,128)} async-done(((f32[1,7392,64]{1,2,0:T(8,128)}), f32[8,7392,64]{1,2,0:T(8,128)}) %all-gather.12.cloned.1.call-update) | async-done | bytes 15138832 | tf_op jit(solution)/shard_map/all_gather | solution.py:33
  750.2 6.3 reduce_sum.28
  758.1 10.3 %psum.61 = f32[64,64]{0,1:T(8,128)S(1)} all-reduce(f32[64,64]{0,1:T(8,128)S(1)} %fusion.27), channel_id=1, replica_groups=mesh['rows'=8,'cols'=4] {'cols'}, use_global_device_ids=true, to_apply=%region_9.13 | all-reduce | flops 4096 | bytes 32768 | tf_op jit(solution)/shard_map/psum | solution.py:35
  768.5 5.8 cholesky.107
  775.9 4.9 custom-call.13
  787.1 11.4 %all-reduce = (f32[64,64]{0,1:T(8,128)S(1)}, f32[64,64]{0,1:T(8,128)S(1)}) all-reduce(f32[64,64]{0,1:T(8,128)S(1)} %convolution_bitcast_fusion.7, f32[64,64]{0,1:T(8,128)S(1)} %convolution_bitcast_fusion.8), channel_id=1, replica_groups=mesh['rows'=8,'cols'=4] {'cols'}, use_global_device_ids=true, to_apply=%region_11.15 | all-reduce | flops 8192 | bytes 65536 | tf_op jit(solution)/shard_map/psum | solution.py:42
  (53 shorter events, 28.3 us)
Async XLA Ops:
  7.2 1.5 copy-start
  7.2 60.9 %all-reduce.4.cloned.1.call-start = ((), (), s32[]{:S(2)}) async-start(), calls=%async_computation | async-start | bytes 524288 | tf_op jit(solution)/shard_map/psum | solution.py:27
  32.9 323.0 %all-gather.10.cloned.1.call-start = ((), (), s32[]{:S(2)}) async-start(), calls=%async_computation.3 | async-start | bytes 17104896 | tf_op jit(solution)/shard_map/all_gather | solution.py:33
  151.4 291.1 %all-reduce.6.cloned.1.call-start = ((), (), s32[]{:S(2)}) async-start(), calls=%async_computation.1 | async-start | bytes 524288 | tf_op jit(solution)/shard_map/psum | solution.py:27
  411.9 129.0 %all-gather.8.cloned.1.call-start = ((), (), s32[]{:S(2)}) async-start(), calls=%async_computation.2 | async-start | bytes 2359296 | tf_op jit(solution)/shard_map/all_gather | solution.py:38
  495.4 254.8 %all-gather.12.cloned.1.call-start = ((), (), s32[]{:S(2)}) async-start(), calls=%async_computation.4 | async-start | bytes 17104896 | tf_op jit(solution)/shard_map/all_gather | solution.py:33
  530.9 10.0 %copy-start.5 = (f32[64,2048]{1,0:T(8,128)S(1)}, f32[64,2048]{1,0:T(8,128)}, u32[]{:S(2)}) copy-start(f32[64,2048]{1,0:T(8,128)} %param.12) | copy-start | bytes 1572868
  756.4 1.6 copy-start.2
  780.8 4.7 copy-start.4
  780.8 19.2 %copy-start.1 = (f32[7392,64]{0,1:T(8,128)S(1)}, f32[7392,64]{0,1:T(8,128)}, u32[]{:S(2)}) copy-start(f32[7392,64]{0,1:T(8,128)} %param.10) | copy-start | bytes 5677060
  784.2 1.3 copy-start.3
Sparse Core Ops, SparseCore 0:
  33.0 34.9 all-reduce.3
  151.6 204.2 all-gather.9
  412.0 30.5 all-reduce.5
  495.5 45.3 all-gather.7
  543.5 206.5 all-gather.11
